TPU v7x, 256 devices: a whole 4x4x8 slice. The times are simulated.
256 devices in a mesh: row: 16 (over z, core), col: 16 (over x, y).
Axes of the slice: x: 4, y: 4, z: 8, core: 2. Of those that a mesh axis runs over, the one named last changes fastest.
Arguments:
- grad: bfloat16 [2, 6144, 24576], P(None, 'row', 'col'), may hold values from -45 to 45, as said below
- memory: float32 [2, 6144, 24576], P(None, 'row', 'col'), may hold values from -6 to 6
- p_prev: float32 [2, 6144, 32], P(None, ('row', 'col')), may hold values from -6 to 6
- q_prev: float32 [2, 24576, 32], P(None, ('col', 'row')), may hold values from -1 to 1
Outputs:
- p_new: float32 [2, 6144, 32], P(None, ('row', 'col'))
- q_new: float32 [2, 24576, 32], P(None, ('col', 'row'))
- error: float32 [2, 6144, 24576], P(None, 'row', 'col')
Inputs may be any that keep to these rules, and one draw needn't show every extreme that they name: `grad`: real-valued gradient entries.
All inputs are finite; a program needn't handle non-finite values.
Results may differ from a plain program's by a relative error of at most 0.0003.
Values sent between devices are 32-bit elements; how exact they have to be, the bound alone decides.
A program may use at most 64 MiB of HBM per device.

v0:
```python
import jax
import jax.numpy as jnp
from jax import lax
from jax.sharding import PartitionSpec as P


def joined_along(pieces, dim):
    shape = list(pieces.shape[1:])
    shape[dim] *= pieces.shape[0]
    return jnp.moveaxis(pieces, 0, dim).reshape(shape)


def sent_to_all(value, axis):
    copies = jnp.broadcast_to(value, (lax.axis_size(axis), *value.shape))
    return lax.all_to_all(copies, axis, split_axis=0, concat_axis=0, tiled=True)


def gathered_copies(value, axis, dim):
    return joined_along(sent_to_all(value, axis), dim)


def over_copies(value, axis):
    return sent_to_all(value, axis).sum(axis=0)


def in_blocks(value, dim, devices):
    before, after = (value.shape[:dim], value.shape[dim + 1 :])
    return jnp.moveaxis(value.reshape(*before, devices, -1, *after), dim, 0)


def summed_on_arrival(value, axis, dim):
    pieces = in_blocks(value, dim, lax.axis_size(axis))
    arrived = lax.all_to_all(pieces, axis, split_axis=0, concat_axis=0, tiled=True)
    return arrived.sum(axis=0)


def shards(grad, memory, p_prev, q_prev):
    highest = lax.Precision.HIGHEST
    left_rows = gathered_copies(p_prev, "col", 1)
    right_rows = lax.all_gather(q_prev, "row", axis=1, tiled=True)
    approx = jnp.einsum("lrk,lck->lrc", left_rows, right_rows, precision=highest)
    merged = grad.astype(jnp.float32) + memory - approx
    partial_value = jnp.einsum("lrc,lck->lrk", merged, right_rows, precision=highest)
    left = over_copies(partial_value, "col")
    gram_part = jnp.einsum("lrk,lrj->lkj", left, left, precision=highest)
    gram = over_copies(gram_part, "row")
    factor = jnp.linalg.cholesky(gram)
    p_hat = lax.linalg.triangular_solve(factor, left, left_side=False, lower=True, transpose_a=True)
    right_part = jnp.einsum("lrc,lrk->lck", merged, p_hat, precision=highest)
    q_new = summed_on_arrival(right_part, "row", 1)
    right_full = gathered_copies(q_new, "row", 1)
    error = merged - jnp.einsum("lrk,lck->lrc", p_hat, right_full, precision=highest)
    left_share = p_hat.shape[1] // lax.axis_size("col")
    p_new = lax.dynamic_slice_in_dim(p_hat, lax.axis_index("col") * left_share, left_share, 1)
    return (p_new, q_new, error)


def solution(mesh):
    placed = (
        P(None, "row", "col"),
        P(None, "row", "col"),
        P(None, ("row", "col"), None),
        P(None, ("col", "row"), None),
    )
    return jax.shard_map(
        shards,
        mesh=mesh,
        in_specs=placed,
        out_specs=(
            P(None, ("row", "col"), None),
            P(None, ("col", "row"), None),
            P(None, "row", "col"),
        ),
        check_vma=False,
    )
```

profile of v0, /device:TPU:1, one launch (start us, length us, event | category | flops | bytes accessed | tf_op | source)
XLA Modules:
  0.0 162.4 jit_solution(4847831025608026556)
XLA Ops:
  0.6 0.8 broadcast_in_dim.16
  1.4 0.8 reshape.28
  2.2 7.6 %all-to-all-start = ((f32[16,1,1536]{2,1,0:T(1,128)}), f32[16,1,1536]{2,1,0:T(1,128)S(1)}, u32[]{:S(2)}, u32[]{:S(2)}) async-start(f32[16,1,1536]{2,1,0:T(1,128)} %reshape.28), calls=%async_computation | async-start | bytes 196608 | tf_op jit(solution)/shard_map/all_to_all | solution.py:15
  9.8 0.9 copy.27
  10.7 25.4 %all_gather.3 = f32[2,1536,32]{2,0,1:T(2,128)S(1)} all-gather(f32[2,96,32]{2,0,1:T(2,128)S(1)} %copy.27), channel_id=1, replica_groups=mesh['row'=16,'col'=16] {'row'}, dimensions={1}, use_global_device_ids=true | all-gather | bytes 417792 | tf_op jit(solution)/shard_map/all_gather | solution.py:40
  36.1 0.6 copy.28
  36.7 0.5 broadcast.47
  37.3 0.9 reduce.6
  38.3 0.3 copy.26
  38.6 0.3 reshape.25
  38.8 6.4 %add_subtract_fusion = f32[2,384,1536]{2,1,0:T(8,128)S(1)} fusion(f32[2,384,1536]{2,1,0:T(8,128)} %param.5, bf16[2,384,1536]{2,1,0:T(8,128)(2,1)} %param.4, f32[2,384,32]{1,2,0:T(8,128)S(1)} %reshape.25, f32[2,1536,32]{1,2,0:T(8,128)S(1)} %copy.28), kind=kOutput, calls=%fused_computation | convolution fusion | flops 456523776 | bytes 12288000 | tf_op jit(solution)/shard_map/lrk,lck->lrc/dot_general | solution.py:41
  45.3 2.2 %copy-done = f32[2,384,1536]{2,1,0:T(8,128)} copy-done((f32[2,384,1536]{2,1,0:T(8,128)}, f32[2,384,1536]{2,1,0:T(8,128)S(1)}, u32[]{:S(2)}) %copy-start) | copy-done | bytes 4718616
  47.4 4.4 %fusion.3 = f32[2,384,32]{1,2,0:T(8,128)S(1)} fusion(f32[2,384,1536]{2,1,0:T(8,128)S(1)} %add_subtract_fusion, f32[2,1536,32]{1,2,0:T(8,128)S(1)} %copy.28), kind=kOutput, calls=%fused_computation.13 | convolution fusion | flops 452984832 | bytes 5210112 | tf_op jit(solution)/shard_map/lrc,lck->lrk/dot_general | solution.py:43
  51.8 0.2 broadcast_in_dim.17
  52.0 28.1 %all_to_all.25 = f32[16,2,384,32]{2,3,1,0:T(8,128)S(1)} all-to-all(f32[16,2,384,32]{2,3,1,0:T(8,128)S(1)} %broadcast_in_dim.17), channel_id=1, replica_groups=mesh['row'=16,'col'=16] {'col'}, dimensions={0} | all-to-all | bytes 3145728 | tf_op jit(solution)/shard_map/all_to_all | solution.py:15
  80.2 0.2 fusion.4
  80.5 0.9 reshape.30
  81.4 5.8 %all-to-all-start.2 = ((f32[16,1,2048]{2,1,0:T(1,128)}), f32[16,1,2048]{2,1,0:T(1,128)S(1)}, u32[]{:S(2)}, u32[]{:S(2)}) async-start(f32[16,1,2048]{2,1,0:T(1,128)} %reshape.30), calls=%async_computation.2 | async-start | bytes 262144 | tf_op jit(solution)/shard_map/all_to_all | solution.py:15
  87.2 8.9 %all-to-all-done.2 = f32[16,1,2048]{2,1,0:T(1,128)S(1)} async-done(((f32[16,1,2048]{2,1,0:T(1,128)}), f32[16,1,2048]{2,1,0:T(1,128)S(1)}, u32[]{:S(2)}, u32[]{:S(2)}) %all-to-all-start.2) | async-done | bytes 131104 | tf_op jit(solution)/shard_map/all_to_all | solution.py:15
  96.1 0.9 reduce.7
  97.3 5.9 %custom-call.7 = f32[2,32,32]{2,1,0:T(8,128)S(1)} custom-call(f32[2,32,32]{2,1,0:T(8,128)S(1)} %fusion.2), custom_call_target="Cholesky" | custom-call | tf_op jit(solution)/shard_map/jit(cholesky)/cholesky | solution.py:47
  103.4 4.9 %custom-call.8 = f32[2,1,32,32]{2,3,1,0:T(8,128)S(1)} custom-call(f32[2,1,32,32]{3,2,1,0:T(8,128)S(1)} %select_bitcast_fusion), custom_call_target="InvertDiagBlocksLowerTriangular" | custom-call | tf_op jit(solution)/shard_map/triangular_solve | solution.py:48
  108.3 0.3 fusion
  108.7 4.7 %fusion.5 = f32[2,1536,32]{1,2,0:T(8,128)S(1)} fusion(f32[2,384,1536]{2,1,0:T(8,128)} %copy-done, f32[2,384,32]{1,2,0:T(8,128)S(1)} %fusion), kind=kOutput, calls=%fused_computation.15 | convolution fusion | flops 452984832 | bytes 5210112 | tf_op jit(solution)/shard_map/lrc,lrk->lck/dot_general | solution.py:49
  113.7 19.9 %all_to_all.26 = f32[16,2,96,32]{2,3,1,0:T(8,128)S(1)} all-to-all(f32[16,2,96,32]{2,3,1,0:T(8,128)S(1)} %bitcast.36), channel_id=1, replica_groups=mesh['row'=16,'col'=16] {'row'}, dimensions={0} | all-to-all | bytes 786432 | tf_op jit(solution)/shard_map/all_to_all | solution.py:33
  133.7 0.8 broadcast_in_dim.19
  134.5 3.5 %all-to-all-start.4 = ((f32[16,2,96,32]{2,3,1,0:T(8,128)}), f32[16,2,96,32]{2,3,1,0:T(8,128)S(1)}, u32[]{:S(2)}, u32[]{:S(2)}) async-start(f32[16,2,96,32]{2,3,1,0:T(8,128)} %broadcast_in_dim.19), calls=%async_computation.4 | async-start | bytes 1048576 | tf_op jit(solution)/shard_map/all_to_all | solution.py:15
  138.1 0.7 copy.34
  138.8 15.9 %all-to-all-done.4 = f32[16,2,96,32]{2,3,1,0:T(8,128)S(1)} async-done(((f32[16,2,96,32]{2,3,1,0:T(8,128)}), f32[16,2,96,32]{2,3,1,0:T(8,128)S(1)}, u32[]{:S(2)}, u32[]{:S(2)}) %all-to-all-start.4) | async-done | bytes 393248 | tf_op jit(solution)/shard_map/all_to_all | solution.py:15
  154.7 0.3 copy.33
  155.0 0.2 reshape.27
  155.2 7.2 %convolution_subtract_fusion = f32[2,384,1536]{2,1,0:T(8,128)} fusion(f32[2,384,1536]{2,1,0:T(8,128)} %copy-done, f32[2,384,32]{1,2,0:T(8,128)S(1)} %fusion, f32[2,1536,32]{1,2,0:T(8,128)S(1)} %reshape.27), kind=kOutput, calls=%fused_computation.1 | convolution fusion | flops 454164480 | bytes 9928704 | tf_op jit(solution)/shard_map/lrk,lck->lrc/dot_general | solution.py:52
  (20 shorter events, 1.3 us)
Async XLA Ops:
  2.2 34.5 %all-to-all-start = ((f32[16,1,1536]{2,1,0:T(1,128)}), f32[16,1,1536]{2,1,0:T(1,128)S(1)}, u32[]{:S(2)}, u32[]{:S(2)}) async-start(f32[16,1,1536]{2,1,0:T(1,128)} %reshape.28), calls=%async_computation | async-start | bytes 196608 | tf_op jit(solution)/shard_map/all_to_all | solution.py:15
  45.2 2.2 %copy-start = (f32[2,384,1536]{2,1,0:T(8,128)}, f32[2,384,1536]{2,1,0:T(8,128)S(1)}, u32[]{:S(2)}) copy-start(f32[2,384,1536]{2,1,0:T(8,128)S(1)} %add_subtract_fusion) | copy-start | bytes 14155780
  81.4 14.6 %all-to-all-start.2 = ((f32[16,1,2048]{2,1,0:T(1,128)}), f32[16,1,2048]{2,1,0:T(1,128)S(1)}, u32[]{:S(2)}, u32[]{:S(2)}) async-start(f32[16,1,2048]{2,1,0:T(1,128)} %reshape.30), calls=%async_computation.2 | async-start | bytes 262144 | tf_op jit(solution)/shard_map/all_to_all | solution.py:15
  133.6 28.8 %copy-start.1 = (f32[2,96,32]{1,2,0:T(8,128)}, f32[2,96,32]{1,2,0:T(8,128)S(1)}, u32[]{:S(2)}) copy-start(f32[2,96,32]{1,2,0:T(8,128)S(1)} %reduce_sum.29) | copy-start | bytes 73732
  134.5 20.2 %all-to-all-start.4 = ((f32[16,2,96,32]{2,3,1,0:T(8,128)}), f32[16,2,96,32]{2,3,1,0:T(8,128)S(1)}, u32[]{:S(2)}, u32[]{:S(2)}) async-start(f32[16,2,96,32]{2,3,1,0:T(8,128)} %broadcast_in_dim.19), calls=%async_computation.4 | async-start | bytes 1048576 | tf_op jit(solution)/shard_map/all_to_all | solution.py:15
where the time goes:
time: 163 us; the launch traced here: 162 us
  blocking collectives  73.4 us (45%)
  waiting for transfers between devices  24.8 us (15%)
  matrix products  23.2 us (14%)
  starting transfers between devices  16.8 us (10%)
  other arithmetic  13 us (8%)
  local copies, waits for them, and re-layouts  10.4 us (6%)
    all_to_all x1, blocking collectives, sent_to_all(): return lax.all_to_all(copies, axis, split_axis=0, concat_axis=0, tiled=True)  28.1 us
    all_gather x1, blocking collectives, shards(): right_rows = lax.all_gather(q_prev, 'row', axis=1, tiled=True)  25.4 us
    all_to_all x3, waiting for transfers between devices, sent_to_all(): return lax.all_to_all(copies, axis, split_axis=0, concat_axis=0, tiled=True)  24.8 us
    all_to_all x1, blocking collectives, summed_on_arrival(): lax.all_to_all(pieces, axis, split_axis=0, concat_axis=0, tiled=True)  19.9 us
    all_to_all x3, starting transfers between devices, sent_to_all(): return lax.all_to_all(copies, axis, split_axis=0, concat_axis=0, tiled=True)  16.8 us
    dot_general x1, matrix products, shards(): jnp.einsum('lrk,lck->lrc', p_hat, right_full, precision=highest)  7.19 us
    dot_general x1, matrix products, shards(): jnp.einsum('lrk,lck->lrc', left_rows, right_rows, precision=highest)  6.4 us
    another operation x4, other arithmetic, shards(): factor = jnp.linalg.cholesky(gram)  6.02 us
  transfers between devices with their start and end apart: 3, of which 2 were waited for; matrix products, arithmetic and copies ran while one was open for 1% of the time, Pallas kernels for 0%

commit v1 on v0

v1 whole, which is shorter than its diff:
```python
import jax
import jax.numpy as jnp
from jax import lax
from jax.experimental import pallas as pl
from jax.experimental.pallas import tpu as pltpu
from jax.sharding import PartitionSpec as P

F32, BF16 = jnp.float32, jnp.bfloat16
HIGHEST = lax.Precision.HIGHEST
NT = (((1,), (1,)), ((), ()))
NN = (((1,), (0,)), ((), ()))
MESH = pl.DeviceIdType.MESH


def dot(a, b, dims=NN, precision=None):
    return lax.dot_general(a, b, dims, precision=precision, preferred_element_type=F32)


def pieces(v):
    first = v.astype(BF16).astype(F32)
    rest = v - first
    second = rest.astype(BF16).astype(F32)
    return first, second, rest - second


def shut(s):
    n = s.shape[1]
    low = jnp.concatenate([s[24:32, i * 32 : i * 32 + 32] for i in range(n // 32)], axis=0)
    return jnp.concatenate([s[0:24], low], axis=1)


def opened(p):
    low = jnp.concatenate([p[8 * i : 8 * i + 8, 96:128] for i in range(3)], axis=1)
    return jnp.concatenate([p[:, 0:96], low], axis=0)


def wide_left(p):
    a, b, c = pieces(p)
    return jnp.concatenate([a, a, a, b, b, c], axis=1).astype(BF16)


def tall_right(q):
    a, b, c = (v.astype(BF16) for v in pieces(q))
    return jnp.concatenate([a, b, c, a, b, a], axis=0)


def factor_kernel(
    zs, xs, ys,
    grad, memory, p_prev, q_prev,
    merged_out, wide_out, right_out, p_new, q_new,
    q_in, p_in, gbuf, tile, hi, lo, qg, pg, p_rows, wide, tall, b1, b2, left, gd, gz, rb, rd, rs, rr,
    load_sem, out_sem, zq_send, zq_recv, dq_send, dq_recv, p_send, p_recv, b_send, b_recv,
    gd_send, gd_recv, gz_send, gz_recv, rd_send, rd_recv, rz_send, rz_recv,
):
    layers, rows, cols = tile.shape
    row, col = lax.axis_index("row"), lax.axis_index("col")
    z, core = row // 2, row % 2
    x, y = col // ys, col % ys
    partner = {"row": z * 2 + (1 - core)}

    def z_peer(d):
        return {"row": ((z + d) % zs) * 2 + core}

    def x_peer(d):
        return {"col": ((x + d) % xs) * ys + y}

    def y_peer(d):
        return {"col": x * ys + (y + d) % ys}

    def remote(src, dst, send, recv, device):
        return pltpu.make_async_remote_copy(
            src_ref=src, dst_ref=dst, send_sem=send, recv_sem=recv, device_id=device, device_id_type=MESH
        )

    sent = []

    def start(copy):
        copy.start()
        sent.append(copy)
        return copy

    load_q = pltpu.make_async_copy(q_prev, q_in, load_sem.at[0])
    load_p = pltpu.make_async_copy(p_prev, p_in, load_sem.at[1])
    load_q.start()
    load_p.start()
    loads = []
    for l in range(layers):
        pair = (
            pltpu.make_async_copy(memory.at[l], tile.at[l], load_sem.at[2 + 2 * l]),
            pltpu.make_async_copy(grad.at[l], gbuf.at[l], load_sem.at[3 + 2 * l]),
        )
        for c in pair:
            c.start()
        loads.append(pair)

    barrier = pltpu.get_barrier_semaphore()
    peers = [partner] + [z_peer(d) for d in range(1, zs)]
    peers += [x_peer(d) for d in range(1, xs)] + [y_peer(d) for d in range(1, ys)]
    for device in peers:
        pl.semaphore_signal(barrier, inc=1, device_id=device, device_id_type=MESH)

    load_q.wait()
    for l in range(layers):
        qg[0, l, row] = shut(q_in[l].T)
    load_p.wait()
    for l in range(layers):
        p = p_in[l]
        pg[x, y, l] = jnp.concatenate([p[0:8], p[8:16], p[16:24], jnp.zeros((8, 32), F32)], axis=1)
    pl.semaphore_wait(barrier, len(peers))

    far_first = sorted(range(1, zs), key=lambda d: -min(d, zs - d))
    near_first = far_first[::-1]

    def send_shards(phase, l):
        mine = qg.at[phase, l, row]
        for d in far_first:
            start(remote(mine, mine, zq_send.at[phase, l, d], zq_recv.at[phase, l, d], z_peer(d)))
        start(remote(mine, mine, dq_send.at[phase, l, 0], dq_recv.at[phase, l, 0], partner))

    def pass_on(phase, l):
        for d in near_first:
            source = ((z + zs - d) % zs) * 2 + core
            there = qg.at[phase, l, source]
            remote(there, there, zq_send.at[phase, l, d], zq_recv.at[phase, l, d], z_peer(d)).wait_recv()
            start(remote(there, there, dq_send.at[phase, l, d], dq_recv.at[phase, l, d], partner))

    def all_passed(phase, l):
        for d in range(zs):
            other = ((z + zs - d) % zs) * 2 + (1 - core)
            there = qg.at[phase, l, other]
            remote(there, there, dq_send.at[phase, l, d], dq_recv.at[phase, l, d], partner).wait_recv()

    send_shards(0, 0)
    for d in range(1, ys):
        mine = pg.at[x, y]
        start(remote(mine, mine, p_send.at[0, d], p_recv.at[0, d], y_peer(d)))
    send_shards(0, 1)

    for l in range(layers):
        for c in loads[l]:
            c.wait()

        @pl.loop(0, rows // 32)
        def _(i):
            at = pl.ds(pl.multiple_of(i * 32, 32), 32)
            tile[l, at, :] = gbuf[l, at, :].astype(F32) + tile[l, at, :]

    for d in range(1, ys):
        there = pg.at[x, (y + ys - d) % ys]
        remote(there, there, p_send.at[0, d], p_recv.at[0, d], y_peer(d)).wait_recv()
    for d in range(1, xs):
        mine = pg.at[x]
        start(remote(mine, mine, p_send.at[1, d], p_recv.at[1, d], x_peer(d)))

    def q_columns(phase, l):
        return jnp.concatenate([opened(qg[phase, l, r]) for r in range(2 * zs)], axis=1)

    def merge(l):
        tall[...] = tall_right(q_columns(0, l))
        p = wide_left(p_rows[l])
        wide[...] = p
        acc = jnp.zeros((rows, 96), F32)
        step = 256
        for j in range(cols // step):
            at = pl.ds(j * step, step)
            m = tile[l, :, at] - dot(wide[...], tall[:, at])
            tile[l, :, at] = m
            m1 = m.astype(BF16)
            m2 = (m - m1.astype(F32)).astype(BF16)
            hi[l, :, at] = m1
            lo[l, :, at] = m2
            acc = acc + dot(m1, tall[0:96, at], NT) + dot(m2, tall[0:96, at], NT)
        part = acc[:, 0:32] + acc[:, 32:64] + acc[:, 64:96]
        return part

    half = rows // 2
    block = half // 4

    def halves(v):
        for h in range(2):
            yield jnp.concatenate([v[h * half + b * block : h * half + (b + 1) * block] for b in range(4)], axis=1)

    def exchange(buf, stage, l, h, along_y):
        n, me, peer = (ys, y, y_peer) if along_y else (xs, x, x_peer)
        mine = buf.at[l, h, me]
        for d in range(1, n):
            start(remote(mine, mine, b_send.at[stage, l, h, d], b_recv.at[stage, l, h, d], peer(d)))

    def arrived(buf, stage, l, h, along_y):
        n, me, peer = (ys, y, y_peer) if along_y else (xs, x, x_peer)
        for d in range(1, n):
            there = buf.at[l, h, (me + n - d) % n]
            remote(there, there, b_send.at[stage, l, h, d], b_recv.at[stage, l, h, d], peer(d)).wait_recv()
        total = buf[l, h, 0]
        for i in range(1, n):
            total = total + buf[l, h, i]
        return total

    def first_stage(l):
        part = merge(l)
        for h, v in enumerate(halves(part)):
            me = y if h == 0 else x
            b1[l, h, me] = v
            exchange(b1, 0, l, h, h == 0)
        pltpu.make_async_copy(tile.at[l], merged_out.at[l], out_sem.at[l]).start()

    def second_stage(l):
        for h in range(2):
            total = arrived(b1, 0, l, h, h == 0)
            me = x if h == 0 else y
            b2[l, h, me] = total
            exchange(b2, 1, l, h, h == 1)

    pass_on(0, 0)
    for d in range(1, xs):
        there = pg.at[(x + xs - d) % xs]
        remote(there, there, p_send.at[1, d], p_recv.at[1, d], x_peer(d)).wait_recv()
    for l in range(layers):
        for c in range(xs * ys):
            v = pg[c // ys, c % ys, l]
            p_rows[l, 24 * c : 24 * c + 24, :] = jnp.concatenate([v[:, 32 * b : 32 * b + 32] for b in range(3)], axis=0)
    all_passed(0, 0)
    first_stage(0)
    pass_on(0, 1)
    all_passed(0, 1)
    first_stage(1)
    second_stage(0)
    second_stage(1)

    def right_part(l):
        for h in range(2):
            total = arrived(b2, 1, l, h, h == 1)
            for b in range(4):
                left[l, h * half + b * block : h * half + (b + 1) * block, :] = total[:, 32 * b : 32 * b + 32]
        v = left[l]
        turned = v.T
        g = dot(turned, v, precision=HIGHEST)
        gd[l, core] = jnp.concatenate([g[8 * i : 8 * i + 8] for i in range(4)], axis=1)
        mine = gd.at[l, core]
        start(remote(mine, mine, gd_send.at[l], gd_recv.at[l], partner))
        t1, t2, t3 = (t.astype(BF16) for t in pieces(turned))
        lhs = jnp.concatenate([t1, t2, t3], axis=0)
        full = dot(lhs, hi[l]) + dot(lhs, lo[l])
        r = full[0:32] + full[32:64] + full[64:96]
        for s in range(2 * zs):
            rb[l, s % 2, s // 2] = shut(r[:, 96 * s : 96 * s + 96])
        start(remote(rb.at[l, 1 - core], rd.at[l], rd_send.at[l], rd_recv.at[l], partner))

    def send_gram(l):
        there = gd.at[l, 1 - core]
        remote(there, there, gd_send.at[l], gd_recv.at[l], partner).wait_recv()
        gz[l, z] = gd[l, 0] + gd[l, 1]
        mine = gz.at[l, z]
        for d in far_first:
            start(remote(mine, mine, gz_send.at[l, d], gz_recv.at[l, d], z_peer(d)))

    def scatter(l):
        remote(rb.at[l, 1 - core], rd.at[l], rd_send.at[l], rd_recv.at[l], partner).wait_recv()
        rs[l] = rb[l, core] + rd[l]
        for d in far_first:
            to = (z + d) % zs
            start(remote(rs.at[l, to], rr.at[l, z], rz_send.at[l, d], rz_recv.at[l, d], z_peer(d)))
        rr[l, z] = rs[l, z]

    right_part(0)
    send_gram(0)
    scatter(0)
    right_part(1)
    send_gram(1)
    scatter(1)

    def whole_gram(l):
        for d in range(1, zs):
            there = gz.at[l, (z + zs - d) % zs]
            remote(there, there, gz_send.at[l, d], gz_recv.at[l, d], z_peer(d)).wait_recv()
        g = gz[l, 0]
        for i in range(1, zs):
            g = g + gz[l, i]
        return jnp.concatenate([g[:, 32 * i : 32 * i + 32] for i in range(4)], axis=0)

    rank = 32
    ri = lax.broadcasted_iota(jnp.int32, (rank, 2 * rank), 0)
    ci = lax.broadcasted_iota(jnp.int32, (rank, 2 * rank), 1)
    eye = jnp.where(ri[:, 0:rank] == ci[:, 0:rank], 1.0, 0.0).astype(F32)
    sides = [jnp.concatenate([whole_gram(l), eye], axis=1) for l in range(layers)]
    for j in range(rank - 1):
        for l in range(layers):
            a = sides[l]
            pivot = a[j : j + 1, :]
            column = a[:, j : j + 1]
            scale = jnp.where(ri[:, 0:1] > j, column / a[j : j + 1, j : j + 1], 0.0)
            sides[l] = a - scale * pivot
    inverses = []
    for a in sides:
        diagonal = jnp.sum(jnp.where(ri == ci, a, 0.0), axis=1, keepdims=True)
        inverses.append(a[:, rank : 2 * rank] * lax.rsqrt(diagonal))

    def finish(l):
        for d in range(1, zs):
            there = rr.at[l, (z + zs - d) % zs]
            remote(rs.at[l, 0], there, rz_send.at[l, d], rz_recv.at[l, d], z_peer(d)).wait_recv()
        total = rr[l, 0]
        for i in range(1, zs):
            total = total + rr[l, i]
        q = dot(inverses[l], opened(total), precision=HIGHEST)
        qg[1, l, row] = shut(q)
        send_shards(1, l)
        q_new[l] = q.T

    finish(0)
    finish(1)
    for l in range(layers):
        p = dot(left[l], inverses[l], NT, precision=HIGHEST)
        p_rows[l] = p
        wide_out[l] = wide_left(p)
        share = rows // (xs * ys)
        p_new[l] = p_rows[l, pl.ds(pl.multiple_of(col * share, 8), share), :]
    for l in range(layers):
        pass_on(1, l)
    for l in range(layers):
        all_passed(1, l)
        right_out[l] = q_columns(1, l)
        pltpu.make_async_copy(tile.at[l], merged_out.at[l], out_sem.at[l]).wait()
    for copy in sent:
        copy.wait_send()


def error_kernel(merged, wide, right, error, buf, tall, in_sem, out_sem):
    layers, rows, cols = buf.shape
    step = 128

    def at(ref, l, i):
        return ref.at[l, pl.ds(i * step, step), :]

    order = [(l, i) for l in range(layers) for i in range(rows // step)]
    ins = [pltpu.make_async_copy(at(merged, l, i), at(buf, l, i), in_sem.at[l, i]) for l, i in order]
    outs = [pltpu.make_async_copy(at(buf, l, i), at(error, l, i), out_sem.at[l, i]) for l, i in order]
    for c in ins:
        c.start()
    for n, (l, i) in enumerate(order):
        if i == 0:
            tall[...] = tall_right(right[l])
        ins[n].wait()
        rows_at = pl.ds(i * step, step)
        buf[l, rows_at, :] = buf[l, rows_at, :] - dot(wide[l, rows_at, :], tall[...])
        outs[n].start()
    for c in outs:
        c.wait()


def shards(xs, ys, zs, grad, memory, p_prev, q_prev):
    layers, rows, cols = grad.shape
    rank = p_prev.shape[2]
    share, wire = q_prev.shape[1], 24
    dma = pltpu.SemaphoreType.DMA
    anywhere = pl.BlockSpec(memory_space=pl.ANY)
    vmem = pl.BlockSpec(memory_space=pltpu.VMEM)
    block = rows // 8

    def body(*refs):
        factor_kernel(zs, xs, ys, *refs)

    merged, wide, right, p_new, q_new = pl.pallas_call(
        body,
        out_shape=(
            jax.ShapeDtypeStruct((layers, rows, cols), F32),
            jax.ShapeDtypeStruct((layers, rows, 6 * rank), BF16),
            jax.ShapeDtypeStruct((layers, rank, cols), F32),
            jax.ShapeDtypeStruct(p_prev.shape, F32),
            jax.ShapeDtypeStruct(q_prev.shape, F32),
        ),
        in_specs=[anywhere] * 4,
        out_specs=(anywhere, vmem, vmem, vmem, vmem),
        scratch_shapes=[
            pltpu.VMEM(q_prev.shape, F32),
            pltpu.VMEM(p_prev.shape, F32),
            pltpu.VMEM((layers, rows, cols), BF16),
            pltpu.VMEM((layers, rows, cols), F32),
            pltpu.VMEM((layers, rows, cols), BF16),
            pltpu.VMEM((layers, rows, cols), BF16),
            pltpu.VMEM((2, layers, 2 * zs, wire, 128), F32),
            pltpu.VMEM((xs, ys, layers, 8, 128), F32),
            pltpu.VMEM((layers, rows, rank), F32),
            pltpu.VMEM((rows, 6 * rank), BF16),
            pltpu.VMEM((6 * rank, cols), BF16),
            pltpu.VMEM((layers, 2, 4, block, 128), F32),
            pltpu.VMEM((layers, 2, 4, block, 128), F32),
            pltpu.VMEM((layers, rows, rank), F32),
            pltpu.VMEM((layers, 2, 8, 128), F32),
            pltpu.VMEM((layers, zs, 8, 128), F32),
            pltpu.VMEM((layers, 2, zs, wire, 128), F32),
            pltpu.VMEM((layers, zs, wire, 128), F32),
            pltpu.VMEM((layers, zs, wire, 128), F32),
            pltpu.VMEM((layers, zs, wire, 128), F32),
            dma((2 + 2 * layers,)),
            dma((layers,)),
            dma((2, layers, zs)),
            dma((2, layers, zs)),
            dma((2, layers, zs)),
            dma((2, layers, zs)),
            dma((2, 4)),
            dma((2, 4)),
            dma((2, layers, 2, 4)),
            dma((2, layers, 2, 4)),
            dma((layers,)),
            dma((layers,)),
            dma((layers, zs)),
            dma((layers, zs)),
            dma((layers,)),
            dma((layers,)),
            dma((layers, zs)),
            dma((layers, zs)),
        ],
        compiler_params=pltpu.CompilerParams(
            collective_id=0, has_side_effects=True, vmem_limit_bytes=48 * 1024 * 1024
        ),
        name="factors",
    )(grad, memory, p_prev, q_prev)
    error = pl.pallas_call(
        error_kernel,
        out_shape=jax.ShapeDtypeStruct((layers, rows, cols), F32),
        in_specs=[anywhere, vmem, vmem],
        out_specs=anywhere,
        scratch_shapes=[
            pltpu.VMEM((layers, rows, cols), F32),
            pltpu.VMEM((6 * rank, cols), BF16),
            dma((layers, rows // 128)),
            dma((layers, rows // 128)),
        ],
        compiler_params=pltpu.CompilerParams(vmem_limit_bytes=32 * 1024 * 1024),
        name="error",
    )(merged, wide, right)
    return p_new, q_new, error


def solution(mesh):
    placed = (
        P(None, "row", "col"),
        P(None, "row", "col"),
        P(None, ("row", "col"), None),
        P(None, ("col", "row"), None),
    )
    xs = ys = 4
    zs = mesh.shape["row"] // 2

    def body(grad, memory, p_prev, q_prev):
        return shards(xs, ys, zs, grad, memory, p_prev, q_prev)

    return jax.shard_map(
        body,
        mesh=mesh,
        in_specs=placed,
        out_specs=(
            P(None, ("row", "col"), None),
            P(None, ("col", "row"), None),
            P(None, "row", "col"),
        ),
        check_vma=False,
    )
```

time: 163 us -> 62.4 us (0.38)
  blocking collectives: 73.4 us -> 0 us
  Pallas kernels: 0 us -> 54.6 us
  waiting for transfers between devices: 24.8 us -> 0 us
  matrix products: 23.2 us -> 0 us
  starting transfers between devices: 16.8 us -> 0 us
  other arithmetic: 13 us -> 0 us
  local copies, waits for them, and re-layouts: 10.4 us -> 6.88 us
    pallas_call x0 -> x2, Pallas kernels: none -> 54.6 us  [the longest x1 51.6 us: shards(): pl.pallas_call(body, out_shape=(jax.ShapeDtypeStruct((layers, rows, cols)...]
    all_to_all x2 -> x0, blocking collectives: 48 us -> none  [the longest x1 28.1 us: sent_to_all(): return lax.all_to_all(copies, axis, split_axis=0, concat_axis=0, tiled=True)]
    all_gather x1 -> x0, blocking collectives: 25.4 us -> none  [shards(): right_rows = lax.all_gather(q_prev, 'row', axis=1, tiled=True)]
    all_to_all x3 -> x0, waiting for transfers between devices: 24.8 us -> none  [sent_to_all(): return lax.all_to_all(copies, axis, split_axis=0, concat_axis=0, tiled=True)]
    dot_general x5 -> x0, matrix products: 22.9 us -> none  [the longest x1 7.19 us: shards(): jnp.einsum('lrk,lck->lrc', p_hat, right_full, precision=highest)]
    all_to_all x3 -> x0, starting transfers between devices: 16.8 us -> none  [sent_to_all(): return lax.all_to_all(copies, axis, split_axis=0, concat_axis=0, tiled=True)]
    another operation x7 -> x0, other arithmetic: 11 us -> none  [the longest x4 6.02 us: shards(): factor = jnp.linalg.cholesky(gram)]
    broadcast_in_dim x4 -> x0, local copies, waits for them, and re-layouts: 1.84 us -> none  [sent_to_all(): copies = jnp.broadcast_to(value, (lax.axis_size(axis), *value.shape))]
  transfers between devices with their start and end apart: 3 -> 0, of which waited for: 2 -> 0; matrix products, arithmetic and copies ran while one was open for 1% -> 0% of each run, Pallas kernels for 0% -> 0%
where the time goes in v1:
time: 62.4 us; the launch traced here: 62.1 us
  Pallas kernels  54.6 us (88%)
  local copies, waits for them, and re-layouts  6.88 us (11%)
  between operations  0.66 us (1%)
    pallas_call x1, Pallas kernels, shards(): pl.pallas_call(body, out_shape=(jax.ShapeDtypeStruct((layers, rows, cols)...  51.6 us
    unnamed x9, local copies, waits for them, and re-layouts  6.88 us
    pallas_call x1, Pallas kernels, shards(): pl.pallas_call(error_kernel, out_shape=jax.ShapeDtypeStruct((layers, rows...  2.94 us

profile of v1, /device:TPU:1, one launch (start us, length us, event | category | flops | bytes accessed | tf_op | source)
XLA Modules:
  0.0 62.1 jit_solution(2930128458099772915)
XLA Ops:
  0.6 0.8 %copy.7.refs_3_ = f32[2,96,32]{2,1,0:T(8,128)S(1)} copy(f32[2,96,32]{1,2,0:T(8,128)} %param.7) | data formatting | bytes 49152 | tf_op args[3]
  1.5 0.0 copy-start.1
  1.5 1.7 %copy-done.1 = bf16[2,384,1536]{2,1,0:T(8,128)(2,1)S(1)} copy-done((bf16[2,384,1536]{2,1,0:T(8,128)(2,1)S(1)}, bf16[2,384,1536]{2,1,0:T(8,128)(2,1)}, u32[]{:S(2)}) %copy-start.1) | copy-done | bytes 2359320
  3.1 0.0 copy-start.2
  3.2 0.7 %copy-done.2 = f32[2,24,32]{2,1,0:T(8,128)S(1)} copy-done((f32[2,24,32]{2,1,0:T(8,128)S(1)}, f32[2,24,32]{2,1,0:T(8,128)}, u32[]{:S(2)}) %copy-start.2) | copy-done | bytes 6168
  3.9 51.6 %factors.1 = (f32[2,384,1536]{2,1,0:T(8,128)}, bf16[2,384,192]{2,1,0:T(8,128)(2,1)S(1)}, f32[2,32,1536]{2,1,0:T(8,128)S(1)}, f32[2,24,32]{2,1,0:T(8,128)S(1)}, f32[2,96,32]{2,1,0:T(8,128)S(1)}) custom-call(bf16[2,384,1536]{2,1,0:T(8,128)(2,1)S(1)} %copy-done.1, f32[2,384,1536]{2,1,0:T(8,128)} %refs_1_.1, f32[2,24,32]{2,1,0:T(8,128)S(1)} %copy-done.2, ...), custom_call_target="tpu_custom_call" | custom-call | tf_op jit(solution)/shard_map/factors/pallas_call | solution.py:363
  55.5 0.7 %copy.8 = f32[2,96,32]{1,2,0:T(8,128)} copy(f32[2,96,32]{2,1,0:T(8,128)S(1)} %get-tuple-element.14) | data formatting | bytes 49152
  56.2 0.0 copy-start
  56.2 2.3 %copy-done = f32[2,384,1536]{2,1,0:T(8,128)S(1)} copy-done((f32[2,384,1536]{2,1,0:T(8,128)S(1)}, f32[2,384,1536]{2,1,0:T(8,128)}, u32[]{:S(2)}) %copy-start) | copy-done | bytes 4718616
  58.5 2.9 %error.1 = f32[2,384,1536]{2,1,0:T(8,128)} custom-call(f32[2,384,1536]{2,1,0:T(8,128)S(1)} %copy-done, bf16[2,384,192]{2,1,0:T(8,128)(2,1)S(1)} %get-tuple-element.11.wide, f32[2,32,1536]{2,1,0:T(8,128)S(1)} %get-tuple-element.12.right), custom_call_target="tpu_custom_call" | custom-call | tf_op jit(solution)/shard_map/error/pallas_call | solution.py:419
  61.5 0.6 copy.10
Async XLA Ops:
  1.5 1.7 %copy-start.1 = (bf16[2,384,1536]{2,1,0:T(8,128)(2,1)S(1)}, bf16[2,384,1536]{2,1,0:T(8,128)(2,1)}, u32[]{:S(2)}) copy-start(bf16[2,384,1536]{2,1,0:T(8,128)(2,1)} %refs_0_.1) | copy-start | bytes 7077892
  3.1 0.7 %copy-start.2 = (f32[2,24,32]{2,1,0:T(8,128)S(1)}, f32[2,24,32]{2,1,0:T(8,128)}, u32[]{:S(2)}) copy-start(f32[2,24,32]{2,1,0:T(8,128)} %refs_2_.1) | copy-start | bytes 18436
  56.2 2.3 %copy-start = (f32[2,384,1536]{2,1,0:T(8,128)S(1)}, f32[2,384,1536]{2,1,0:T(8,128)}, u32[]{:S(2)}) copy-start(f32[2,384,1536]{2,1,0:T(8,128)} %get-tuple-element.10.merged) | copy-start | bytes 14155780

commit v2 on v1

--- a/solution.py
+++ b/solution.py
@@ -47,9 +47,9 @@
 def factor_kernel(
     zs, xs, ys,
     grad, memory, p_prev, q_prev,
-    merged_out, wide_out, right_out, p_new, q_new,
-    q_in, p_in, gbuf, tile, hi, lo, qg, pg, p_rows, wide, tall, b1, b2, left, gd, gz, rb, rd, rs, rr,
-    load_sem, out_sem, zq_send, zq_recv, dq_send, dq_recv, p_send, p_recv, b_send, b_recv,
+    tile, wide_out, right_out, p_new, q_new,
+    q_in, p_in, gbuf, hi, lo, qg, pg, p_rows, wide, tall, b1, b2, left, gd, gz, rb, rd, rs, rr,
+    load_sem, zq_send, zq_recv, dq_send, dq_recv, p_send, p_recv, b_send, b_recv,
     gd_send, gd_recv, gz_send, gz_recv, rd_send, rd_recv, rz_send, rz_recv,
 ):
     layers, rows, cols = tile.shape
@@ -61,6 +61,9 @@
     def z_peer(d):
         return {"row": ((z + d) % zs) * 2 + core}
 
+    def xy_peer(dx, dy):
+        return {"col": lax.rem(x + dx, xs) * ys + lax.rem(y + dy, ys)}
+
     def x_peer(d):
         return {"col": ((x + d) % xs) * ys + y}
 
@@ -95,17 +98,31 @@
 
     barrier = pltpu.get_barrier_semaphore()
     peers = [partner] + [z_peer(d) for d in range(1, zs)]
-    peers += [x_peer(d) for d in range(1, xs)] + [y_peer(d) for d in range(1, ys)]
+    offsets = [(dx, dy) for dx in (2, 1, 3, 0) for dy in (2, 1, 3, 0) if dx or dy]
+    peers += [xy_peer(dx, dy) for dx, dy in offsets]
     for device in peers:
         pl.semaphore_signal(barrier, inc=1, device_id=device, device_id_type=MESH)
 
     load_q.wait()
     for l in range(layers):
-        qg[0, l, row] = shut(q_in[l].T)
+        qg[0, l, row] = shut(q_in[l])
     load_p.wait()
     for l in range(layers):
         p = p_in[l]
         pg[x, y, l] = jnp.concatenate([p[0:8], p[8:16], p[16:24], jnp.zeros((8, 32), F32)], axis=1)
+    for l in range(layers):
+        for c in loads[l]:
+            c.wait()
+
+        @pl.loop(0, rows // 32)
+        def _(i):
+            at = pl.ds(pl.multiple_of(i * 32, 32), 32)
+            t = gbuf[l, at, :].astype(F32) + tile[l, at, :]
+            tile[l, at, :] = t
+            t1 = t.astype(BF16)
+            hi[l, at, :] = t1
+            lo[l, at, :] = (t - t1.astype(F32)).astype(BF16)
+
     pl.semaphore_wait(barrier, len(peers))
 
     far_first = sorted(range(1, zs), key=lambda d: -min(d, zs - d))
@@ -131,47 +148,35 @@
             remote(there, there, dq_send.at[phase, l, d], dq_recv.at[phase, l, d], partner).wait_recv()
 
     send_shards(0, 0)
-    for d in range(1, ys):
+    for dx, dy in offsets:
         mine = pg.at[x, y]
-        start(remote(mine, mine, p_send.at[0, d], p_recv.at[0, d], y_peer(d)))
+        start(remote(mine, mine, p_send.at[dx, dy], p_recv.at[dx, dy], xy_peer(dx, dy)))
     send_shards(0, 1)
-
-    for l in range(layers):
-        for c in loads[l]:
-            c.wait()
-
-        @pl.loop(0, rows // 32)
-        def _(i):
-            at = pl.ds(pl.multiple_of(i * 32, 32), 32)
-            tile[l, at, :] = gbuf[l, at, :].astype(F32) + tile[l, at, :]
-
-    for d in range(1, ys):
-        there = pg.at[x, (y + ys - d) % ys]
-        remote(there, there, p_send.at[0, d], p_recv.at[0, d], y_peer(d)).wait_recv()
-    for d in range(1, xs):
-        mine = pg.at[x]
-        start(remote(mine, mine, p_send.at[1, d], p_recv.at[1, d], x_peer(d)))
 
     def q_columns(phase, l):
         return jnp.concatenate([opened(qg[phase, l, r]) for r in range(2 * zs)], axis=1)
 
+    step = 256
+
+    def left_part(l):
+        tall[l] = tall_right(q_columns(0, l))
+        wide[l] = wide_left(p_rows[l])
+        q3 = tall[l, 0:96, :]
+        acc = dot(hi[l], q3, NT) + dot(lo[l], q3, NT)
+        square = dot(q3, q3, NT)
+        square = square[0:32] + square[32:64] + square[64:96]
+        square = square[:, 0:32] + square[:, 32:64] + square[:, 64:96]
+        part = acc[:, 0:32] + acc[:, 32:64] + acc[:, 64:96]
+        return part - dot(wide[l], tall_right(square))
+
     def merge(l):
-        tall[...] = tall_right(q_columns(0, l))
-        p = wide_left(p_rows[l])
-        wide[...] = p
-        acc = jnp.zeros((rows, 96), F32)
-        step = 256
         for j in range(cols // step):
             at = pl.ds(j * step, step)
-            m = tile[l, :, at] - dot(wide[...], tall[:, at])
+            m = tile[l, :, at] - dot(wide[l], tall[l, :, at])
             tile[l, :, at] = m
             m1 = m.astype(BF16)
-            m2 = (m - m1.astype(F32)).astype(BF16)
             hi[l, :, at] = m1
-            lo[l, :, at] = m2
-            acc = acc + dot(m1, tall[0:96, at], NT) + dot(m2, tall[0:96, at], NT)
-        part = acc[:, 0:32] + acc[:, 32:64] + acc[:, 64:96]
-        return part
+            lo[l, :, at] = (m - m1.astype(F32)).astype(BF16)
 
     half = rows // 2
     block = half // 4
@@ -197,12 +202,11 @@
         return total
 
     def first_stage(l):
-        part = merge(l)
+        part = left_part(l)
         for h, v in enumerate(halves(part)):
             me = y if h == 0 else x
             b1[l, h, me] = v
             exchange(b1, 0, l, h, h == 0)
-        pltpu.make_async_copy(tile.at[l], merged_out.at[l], out_sem.at[l]).start()
 
     def second_stage(l):
         for h in range(2):
@@ -212,18 +216,20 @@
             exchange(b2, 1, l, h, h == 1)
 
     pass_on(0, 0)
-    for d in range(1, xs):
-        there = pg.at[(x + xs - d) % xs]
-        remote(there, there, p_send.at[1, d], p_recv.at[1, d], x_peer(d)).wait_recv()
+    for dx, dy in offsets[::-1]:
+        there = pg.at[lax.rem(x + xs - dx, xs), lax.rem(y + ys - dy, ys)]
+        remote(there, there, p_send.at[dx, dy], p_recv.at[dx, dy], xy_peer(dx, dy)).wait_recv()
     for l in range(layers):
         for c in range(xs * ys):
             v = pg[c // ys, c % ys, l]
             p_rows[l, 24 * c : 24 * c + 24, :] = jnp.concatenate([v[:, 32 * b : 32 * b + 32] for b in range(3)], axis=0)
+    pass_on(0, 1)
     all_passed(0, 0)
     first_stage(0)
-    pass_on(0, 1)
     all_passed(0, 1)
     first_stage(1)
+    merge(0)
+    merge(1)
     second_stage(0)
     second_stage(1)
 
@@ -264,10 +270,23 @@
 
     right_part(0)
     send_gram(0)
+    right_part(1)
     scatter(0)
-    right_part(1)
     send_gram(1)
     scatter(1)
+
+    def gather(l):
+        for d in near_first:
+            there = rr.at[l, (z + zs - d) % zs]
+            remote(rs.at[l, 0], there, rz_send.at[l, d], rz_recv.at[l, d], z_peer(d)).wait_recv()
+        total = rr[l, 0]
+        for i in range(1, zs):
+            total = total + rr[l, i]
+        qg[1, l, row] = total
+        send_shards(1, l)
+
+    gather(0)
+    gather(1)
 
     def whole_gram(l):
         for d in range(1, zs):
@@ -295,65 +314,53 @@
         diagonal = jnp.sum(jnp.where(ri == ci, a, 0.0), axis=1, keepdims=True)
         inverses.append(a[:, rank : 2 * rank] * lax.rsqrt(diagonal))
 
-    def finish(l):
-        for d in range(1, zs):
-            there = rr.at[l, (z + zs - d) % zs]
-            remote(rs.at[l, 0], there, rz_send.at[l, d], rz_recv.at[l, d], z_peer(d)).wait_recv()
-        total = rr[l, 0]
-        for i in range(1, zs):
-            total = total + rr[l, i]
-        q = dot(inverses[l], opened(total), precision=HIGHEST)
-        qg[1, l, row] = shut(q)
-        send_shards(1, l)
-        q_new[l] = q.T
-
-    finish(0)
-    finish(1)
     for l in range(layers):
         p = dot(left[l], inverses[l], NT, precision=HIGHEST)
         p_rows[l] = p
-        wide_out[l] = wide_left(p)
+        wide_out[l] = wide_left(dot(p, inverses[l], precision=HIGHEST))
         share = rows // (xs * ys)
         p_new[l] = p_rows[l, pl.ds(pl.multiple_of(col * share, 8), share), :]
+        q_new[l] = dot(inverses[l], opened(qg[1, l, row]), precision=HIGHEST)
+    for copy in sent:
+        copy.wait_send()
+    sent.clear()
     for l in range(layers):
         pass_on(1, l)
     for l in range(layers):
         all_passed(1, l)
         right_out[l] = q_columns(1, l)
-        pltpu.make_async_copy(tile.at[l], merged_out.at[l], out_sem.at[l]).wait()
     for copy in sent:
         copy.wait_send()
 
 
-def error_kernel(merged, wide, right, error, buf, tall, in_sem, out_sem):
+def error_kernel(merged, wide, right, p_in, q_in, p_new, q_new, error, buf, tall, out_sem, small_sem):
     layers, rows, cols = buf.shape
     step = 128
-
-    def at(ref, l, i):
-        return ref.at[l, pl.ds(i * step, step), :]
-
-    order = [(l, i) for l in range(layers) for i in range(rows // step)]
-    ins = [pltpu.make_async_copy(at(merged, l, i), at(buf, l, i), in_sem.at[l, i]) for l, i in order]
-    outs = [pltpu.make_async_copy(at(buf, l, i), at(error, l, i), out_sem.at[l, i]) for l, i in order]
-    for c in ins:
+    small = [
+        pltpu.make_async_copy(p_in, p_new, small_sem.at[0]),
+        pltpu.make_async_copy(q_in, q_new, small_sem.at[1]),
+    ]
+    for c in small:
         c.start()
-    for n, (l, i) in enumerate(order):
-        if i == 0:
-            tall[...] = tall_right(right[l])
-        ins[n].wait()
-        rows_at = pl.ds(i * step, step)
-        buf[l, rows_at, :] = buf[l, rows_at, :] - dot(wide[l, rows_at, :], tall[...])
-        outs[n].start()
-    for c in outs:
+    outs = []
+    for l in range(layers):
+        tall[...] = tall_right(right[l])
+        for i in range(rows // step):
+            at = pl.ds(i * step, step)
+            buf[l, at, :] = merged[l, at, :] - dot(wide[l, at, :], tall[...])
+            copy = pltpu.make_async_copy(buf.at[l, at, :], error.at[l, at, :], out_sem.at[l, i])
+            copy.start()
+            outs.append(copy)
+    for c in outs + small:
         c.wait()
 
 
 def shards(xs, ys, zs, grad, memory, p_prev, q_prev):
     layers, rows, cols = grad.shape
     rank = p_prev.shape[2]
-    share, wire = q_prev.shape[1], 24
+    wire = 24
     dma = pltpu.SemaphoreType.DMA
-    anywhere = pl.BlockSpec(memory_space=pl.ANY)
+    hbm = pl.BlockSpec(memory_space=pltpu.HBM)
     vmem = pl.BlockSpec(memory_space=pltpu.VMEM)
     block = rows // 8
 
@@ -369,20 +376,19 @@
             jax.ShapeDtypeStruct(p_prev.shape, F32),
             jax.ShapeDtypeStruct(q_prev.shape, F32),
         ),
-        in_specs=[anywhere] * 4,
-        out_specs=(anywhere, vmem, vmem, vmem, vmem),
+        in_specs=[hbm] * 4,
+        out_specs=(vmem,) * 5,
         scratch_shapes=[
             pltpu.VMEM(q_prev.shape, F32),
             pltpu.VMEM(p_prev.shape, F32),
             pltpu.VMEM((layers, rows, cols), BF16),
-            pltpu.VMEM((layers, rows, cols), F32),
             pltpu.VMEM((layers, rows, cols), BF16),
             pltpu.VMEM((layers, rows, cols), BF16),
             pltpu.VMEM((2, layers, 2 * zs, wire, 128), F32),
             pltpu.VMEM((xs, ys, layers, 8, 128), F32),
             pltpu.VMEM((layers, rows, rank), F32),
-            pltpu.VMEM((rows, 6 * rank), BF16),
-            pltpu.VMEM((6 * rank, cols), BF16),
+            pltpu.VMEM((layers, rows, 6 * rank), BF16),
+            pltpu.VMEM((layers, 6 * rank, cols), BF16),
             pltpu.VMEM((layers, 2, 4, block, 128), F32),
             pltpu.VMEM((layers, 2, 4, block, 128), F32),
             pltpu.VMEM((layers, rows, rank), F32),
@@ -393,13 +399,12 @@
             pltpu.VMEM((layers, zs, wire, 128), F32),
             pltpu.VMEM((layers, zs, wire, 128), F32),
             dma((2 + 2 * layers,)),
-            dma((layers,)),
             dma((2, layers, zs)),
             dma((2, layers, zs)),
             dma((2, layers, zs)),
             dma((2, layers, zs)),
-            dma((2, 4)),
-            dma((2, 4)),
+            dma((xs, ys)),
+            dma((xs, ys)),
             dma((2, layers, 2, 4)),
             dma((2, layers, 2, 4)),
             dma((layers,)),
@@ -412,25 +417,28 @@
             dma((layers, zs)),
         ],
         compiler_params=pltpu.CompilerParams(
-            collective_id=0, has_side_effects=True, vmem_limit_bytes=48 * 1024 * 1024
+            collective_id=0, has_side_effects=True, vmem_limit_bytes=28 * 1024 * 1024
         ),
         name="factors",
-    )(grad, memory, p_prev, q_prev)
-    error = pl.pallas_call(
+    )(*(pltpu.with_memory_space_constraint(v, pltpu.HBM) for v in (grad, memory, p_prev, q_prev)))
+    return pl.pallas_call(
         error_kernel,
-        out_shape=jax.ShapeDtypeStruct((layers, rows, cols), F32),
-        in_specs=[anywhere, vmem, vmem],
-        out_specs=anywhere,
+        out_shape=(
+            jax.ShapeDtypeStruct(p_prev.shape, F32),
+            jax.ShapeDtypeStruct(q_prev.shape, F32),
+            jax.ShapeDtypeStruct((layers, rows, cols), F32),
+        ),
+        in_specs=[vmem] * 5,
+        out_specs=(hbm,) * 3,
         scratch_shapes=[
             pltpu.VMEM((layers, rows, cols), F32),
             pltpu.VMEM((6 * rank, cols), BF16),
             dma((layers, rows // 128)),
-            dma((layers, rows // 128)),
+            dma((2,)),
         ],
         compiler_params=pltpu.CompilerParams(vmem_limit_bytes=32 * 1024 * 1024),
         name="error",
-    )(merged, wide, right)
-    return p_new, q_new, error
+    )(merged, wide, right, p_new, q_new)
 
 
 def solution(mesh):
@@ -444,7 +452,8 @@
     zs = mesh.shape["row"] // 2
 
     def body(grad, memory, p_prev, q_prev):
-        return shards(xs, ys, zs, grad, memory, p_prev, q_prev)
+        p_new, q_new, error = shards(xs, ys, zs, grad, memory, p_prev, jnp.swapaxes(q_prev, 1, 2))
+        return p_new, jnp.swapaxes(q_new, 1, 2), error
 
     return jax.shard_map(
         body,

time: 62.4 us -> 51.7 us (0.83)
  local copies, waits for them, and re-layouts: 6.88 us -> 0 us
  Pallas kernels: 54.6 us -> 51 us
    unnamed x9 -> x0, local copies, waits for them, and re-layouts: 6.88 us -> none
    pallas_call x1, Pallas kernels: 51.6 us -> 48.5 us  [shards(): pl.pallas_call(body, out_shape=(jax.ShapeDtypeStruct((layers, rows, cols)...]
where the time goes in v2:
time: 51.7 us
  Pallas kernels  51 us (99%)
  between operations  0.64 us (1%)
    pallas_call x1, Pallas kernels, shards(): pl.pallas_call(body, out_shape=(jax.ShapeDtypeStruct((layers, rows, cols)...  48.5 us
    pallas_call x1, Pallas kernels, shards(): pl.pallas_call(error_kernel, out_shape=(jax.ShapeDtypeStruct(p_prev.shape...  2.53 us

profile of v2, /device:TPU:1, one launch (start us, length us, event | category | flops | bytes accessed | tf_op | source)
XLA Modules:
  0.0 51.7 jit_solution(11252890175580298477)
XLA Ops:
  0.6 48.5 %factors.1 = (f32[2,384,1536]{2,1,0:T(8,128)S(1)}, bf16[2,384,192]{2,1,0:T(8,128)(2,1)S(1)}, f32[2,32,1536]{2,1,0:T(8,128)S(1)}, f32[2,24,32]{2,1,0:T(8,128)S(1)}, f32[2,32,96]{2,1,0:T(8,128)S(1)}) custom-call(bf16[2,384,1536]{2,1,0:T(8,128)(2,1)} %refs_0_.1, f32[2,384,1536]{2,1,0:T(8,128)} %refs_1_.1, f32[2,24,32]{2,1,0:T(8,128)} %refs_2_.1, ...), custom_call_target="tpu_custom_call" | custom-call | tf_op jit(solution)/shard_map/factors/pallas_call | solution.py:370
  49.1 2.5 %error.1 = (f32[2,24,32]{2,1,0:T(8,128)}, f32[2,32,96]{2,1,0:T(8,128)}, f32[2,384,1536]{2,1,0:T(8,128)}) custom-call(f32[2,384,1536]{2,1,0:T(8,128)S(1)} %get-tuple-element.11.merged, bf16[2,384,192]{2,1,0:T(8,128)(2,1)S(1)} %get-tuple-element.12.wide, f32[2,32,1536]{2,1,0:T(8,128)S(1)} %get-tuple-element.13.right, f32[2,24,32]{2,1,0:T(8,128)S(1)} %get-tuple-element.14.p_in, ...), custom_call_target="tpu_custom_call" | custom-call | tf_op jit(solution)/shard_map/error/pallas_call | solution.py:424

commit v3 on v2

--- a/solution.py
+++ b/solution.py
@@ -6,14 +6,13 @@
 from jax.sharding import PartitionSpec as P
 
 F32, BF16 = jnp.float32, jnp.bfloat16
-HIGHEST = lax.Precision.HIGHEST
 NT = (((1,), (1,)), ((), ()))
 NN = (((1,), (0,)), ((), ()))
 MESH = pl.DeviceIdType.MESH
 
 
-def dot(a, b, dims=NN, precision=None):
-    return lax.dot_general(a, b, dims, precision=precision, preferred_element_type=F32)
+def dot(a, b, dims=NN):
+    return lax.dot_general(a, b, dims, preferred_element_type=F32)
 
 
 def pieces(v):
@@ -44,11 +43,45 @@
     return jnp.concatenate([a, b, c, a, b, a], axis=0)
 
 
+def wide_right(q):
+    a, b, c = pieces(q)
+    return jnp.concatenate([a, b, c, a, b, a], axis=1).astype(BF16)
+
+
+def folded(v):
+    v = v[0:32] + v[32:64] + v[64:96]
+    return v[:, 0:32] + v[:, 32:64] + v[:, 64:96]
+
+
+def inverse_factors(grams):
+    n, panel = grams[0].shape[0], 8
+    ri = lax.broadcasted_iota(jnp.int32, (n, 2 * n), 0)
+    ci = lax.broadcasted_iota(jnp.int32, (n, 2 * n), 1)
+    eye = jnp.where(ri[:, 0:n] == ci[:, 0:n], 1.0, 0.0).astype(F32)
+    sides = [jnp.concatenate([g, eye], axis=1) for g in grams]
+    roots = [jnp.zeros((n, 2 * n), F32) for g in grams]
+    for first in range(0, n, panel):
+        columns = [
+            [jnp.broadcast_to(a[:, first + k : first + k + 1], (n, 2 * n)) for k in range(panel)] for a in sides
+        ]
+        for k in range(panel):
+            j = first + k
+            for i in range(len(sides)):
+                own = columns[i][k]
+                pivot = own[j : j + 1, :]
+                roots[i] = jnp.where(ri == j, pivot, roots[i])
+                scale = jnp.where(ri > j, own * (1.0 / pivot), 0.0)
+                for other in range(k + 1, panel):
+                    columns[i][other] = columns[i][other] - scale * columns[i][other][j : j + 1, :]
+                sides[i] = sides[i] - scale * sides[i][j : j + 1, :]
+    return [(a * lax.rsqrt(r))[:, n : 2 * n] for a, r in zip(sides, roots)]
+
+
 def factor_kernel(
     zs, xs, ys,
     grad, memory, p_prev, q_prev,
     tile, wide_out, right_out, p_new, q_new,
-    q_in, p_in, gbuf, hi, lo, qg, pg, p_rows, wide, tall, b1, b2, left, gd, gz, rb, rd, rs, rr,
+    q_in, p_in, gbuf, split, qg, pg, p_rows, wide, tall, b1, b2, left, gd, gz, rb, rd, rs, rr,
     load_sem, zq_send, zq_recv, dq_send, dq_recv, p_send, p_recv, b_send, b_recv,
     gd_send, gd_recv, gz_send, gz_recv, rd_send, rd_recv, rz_send, rz_recv,
 ):
@@ -105,7 +138,7 @@
 
     load_q.wait()
     for l in range(layers):
-        qg[0, l, row] = shut(q_in[l])
+        qg[0, row, l] = shut(q_in[l])
     load_p.wait()
     for l in range(layers):
         p = p_in[l]
@@ -120,54 +153,60 @@
             t = gbuf[l, at, :].astype(F32) + tile[l, at, :]
             tile[l, at, :] = t
             t1 = t.astype(BF16)
-            hi[l, at, :] = t1
-            lo[l, at, :] = (t - t1.astype(F32)).astype(BF16)
+            split[l, at, :] = t1
+            split[l, pl.ds(pl.multiple_of(rows + i * 32, 32), 32), :] = (t - t1.astype(F32)).astype(BF16)
 
     pl.semaphore_wait(barrier, len(peers))
 
     far_first = sorted(range(1, zs), key=lambda d: -min(d, zs - d))
     near_first = far_first[::-1]
 
-    def send_shards(phase, l):
-        mine = qg.at[phase, l, row]
+    def shard(phase, l, slot):
+        return qg.at[phase, slot] if l is None else qg.at[phase, slot, l]
+
+    def send_shards(phase, l=None):
+        mine, i = shard(phase, l, row), l or 0
         for d in far_first:
-            start(remote(mine, mine, zq_send.at[phase, l, d], zq_recv.at[phase, l, d], z_peer(d)))
-        start(remote(mine, mine, dq_send.at[phase, l, 0], dq_recv.at[phase, l, 0], partner))
-
-    def pass_on(phase, l):
+            start(remote(mine, mine, zq_send.at[phase, i, d], zq_recv.at[phase, i, d], z_peer(d)))
+        start(remote(mine, mine, dq_send.at[phase, i, 0], dq_recv.at[phase, i, 0], partner))
+
+    def pass_on(phase, l=None):
+        i = l or 0
         for d in near_first:
-            source = ((z + zs - d) % zs) * 2 + core
-            there = qg.at[phase, l, source]
-            remote(there, there, zq_send.at[phase, l, d], zq_recv.at[phase, l, d], z_peer(d)).wait_recv()
-            start(remote(there, there, dq_send.at[phase, l, d], dq_recv.at[phase, l, d], partner))
-
-    def all_passed(phase, l):
+            there = shard(phase, l, lax.rem(z + zs - d, zs) * 2 + core)
+            remote(there, there, zq_send.at[phase, i, d], zq_recv.at[phase, i, d], z_peer(d)).wait_recv()
+            start(remote(there, there, dq_send.at[phase, i, d], dq_recv.at[phase, i, d], partner))
+
+    def all_passed(phase, l=None):
+        i = l or 0
         for d in range(zs):
-            other = ((z + zs - d) % zs) * 2 + (1 - core)
-            there = qg.at[phase, l, other]
-            remote(there, there, dq_send.at[phase, l, d], dq_recv.at[phase, l, d], partner).wait_recv()
-
-    send_shards(0, 0)
+            there = shard(phase, l, lax.rem(z + zs - d, zs) * 2 + (1 - core))
+            remote(there, there, dq_send.at[phase, i, d], dq_recv.at[phase, i, d], partner).wait_recv()
+
+    send_shards(0)
     for dx, dy in offsets:
         mine = pg.at[x, y]
         start(remote(mine, mine, p_send.at[dx, dy], p_recv.at[dx, dy], xy_peer(dx, dy)))
-    send_shards(0, 1)
 
     def q_columns(phase, l):
-        return jnp.concatenate([opened(qg[phase, l, r]) for r in range(2 * zs)], axis=1)
+        return jnp.concatenate([opened(qg[phase, r, l]) for r in range(2 * zs)], axis=1)
 
     step = 256
+    half = rows // 2
+    block = half // 4
 
     def left_part(l):
         tall[l] = tall_right(q_columns(0, l))
         wide[l] = wide_left(p_rows[l])
         q3 = tall[l, 0:96, :]
-        acc = dot(hi[l], q3, NT) + dot(lo[l], q3, NT)
         square = dot(q3, q3, NT)
-        square = square[0:32] + square[32:64] + square[64:96]
-        square = square[:, 0:32] + square[:, 32:64] + square[:, 64:96]
-        part = acc[:, 0:32] + acc[:, 32:64] + acc[:, 64:96]
-        return part - dot(wide[l], tall_right(square))
+        parts = []
+        for h in range(2):
+            first, second = (split[l, i * rows + h * half : i * rows + (h + 1) * half, :] for i in range(2))
+            acc = dot(first, q3, NT) + dot(second, q3, NT)
+            parts.append(acc[:, 0:32] + acc[:, 32:64] + acc[:, 64:96])
+        less = dot(wide[l], tall_right(folded(square)))
+        return jnp.concatenate(parts, axis=0) - less
 
     def merge(l):
         for j in range(cols // step):
@@ -175,11 +214,8 @@
             m = tile[l, :, at] - dot(wide[l], tall[l, :, at])
             tile[l, :, at] = m
             m1 = m.astype(BF16)
-            hi[l, :, at] = m1
-            lo[l, :, at] = (m - m1.astype(F32)).astype(BF16)
-
-    half = rows // 2
-    block = half // 4
+            split[l, 0:rows, at] = m1
+            split[l, rows : 2 * rows, at] = (m - m1.astype(F32)).astype(BF16)
 
     def halves(v):
         for h in range(2):
@@ -215,7 +251,7 @@
             b2[l, h, me] = total
             exchange(b2, 1, l, h, h == 1)
 
-    pass_on(0, 0)
+    pass_on(0)
     for dx, dy in offsets[::-1]:
         there = pg.at[lax.rem(x + xs - dx, xs), lax.rem(y + ys - dy, ys)]
         remote(there, there, p_send.at[dx, dy], p_recv.at[dx, dy], xy_peer(dx, dy)).wait_recv()
@@ -223,10 +259,8 @@
         for c in range(xs * ys):
             v = pg[c // ys, c % ys, l]
             p_rows[l, 24 * c : 24 * c + 24, :] = jnp.concatenate([v[:, 32 * b : 32 * b + 32] for b in range(3)], axis=0)
-    pass_on(0, 1)
-    all_passed(0, 0)
+    all_passed(0)
     first_stage(0)
-    all_passed(0, 1)
     first_stage(1)
     merge(0)
     merge(1)
@@ -238,15 +272,13 @@
             total = arrived(b2, 1, l, h, h == 1)
             for b in range(4):
                 left[l, h * half + b * block : h * half + (b + 1) * block, :] = total[:, 32 * b : 32 * b + 32]
-        v = left[l]
-        turned = v.T
-        g = dot(turned, v, precision=HIGHEST)
+        t1, t2, t3 = (t.astype(BF16) for t in pieces(left[l].T))
+        lhs = jnp.concatenate([t1, t2, t3], axis=0)
+        g = folded(dot(lhs, lhs, NT))
         gd[l, core] = jnp.concatenate([g[8 * i : 8 * i + 8] for i in range(4)], axis=1)
         mine = gd.at[l, core]
         start(remote(mine, mine, gd_send.at[l], gd_recv.at[l], partner))
-        t1, t2, t3 = (t.astype(BF16) for t in pieces(turned))
-        lhs = jnp.concatenate([t1, t2, t3], axis=0)
-        full = dot(lhs, hi[l]) + dot(lhs, lo[l])
+        full = dot(lhs, split[l, 0:rows, :]) + dot(lhs, split[l, rows : 2 * rows, :])
         r = full[0:32] + full[32:64] + full[64:96]
         for s in range(2 * zs):
             rb[l, s % 2, s // 2] = shut(r[:, 96 * s : 96 * s + 96])
@@ -270,10 +302,10 @@
 
     right_part(0)
     send_gram(0)
+    scatter(0)
     right_part(1)
-    scatter(0)
+    scatter(1)
     send_gram(1)
-    scatter(1)
 
     def gather(l):
         for d in near_first:
@@ -282,7 +314,7 @@
         total = rr[l, 0]
         for i in range(1, zs):
             total = total + rr[l, i]
-        qg[1, l, row] = total
+        qg[1, row, l] = total
         send_shards(1, l)
 
     gather(0)
@@ -297,30 +329,18 @@
             g = g + gz[l, i]
         return jnp.concatenate([g[:, 32 * i : 32 * i + 32] for i in range(4)], axis=0)
 
-    rank = 32
-    ri = lax.broadcasted_iota(jnp.int32, (rank, 2 * rank), 0)
-    ci = lax.broadcasted_iota(jnp.int32, (rank, 2 * rank), 1)
-    eye = jnp.where(ri[:, 0:rank] == ci[:, 0:rank], 1.0, 0.0).astype(F32)
-    sides = [jnp.concatenate([whole_gram(l), eye], axis=1) for l in range(layers)]
-    for j in range(rank - 1):
-        for l in range(layers):
-            a = sides[l]
-            pivot = a[j : j + 1, :]
-            column = a[:, j : j + 1]
-            scale = jnp.where(ri[:, 0:1] > j, column / a[j : j + 1, j : j + 1], 0.0)
-            sides[l] = a - scale * pivot
-    inverses = []
-    for a in sides:
-        diagonal = jnp.sum(jnp.where(ri == ci, a, 0.0), axis=1, keepdims=True)
-        inverses.append(a[:, rank : 2 * rank] * lax.rsqrt(diagonal))
-
-    for l in range(layers):
-        p = dot(left[l], inverses[l], NT, precision=HIGHEST)
+    for l in range(layers):
+        wide[l] = wide_left(left[l])
+    inverses = inverse_factors([whole_gram(l) for l in range(layers)])
+    for l in range(layers):
+        inverse = inverses[l]
+        tall_inverse = tall_right(inverse)
+        p = dot(wide[l], wide_right(inverse), NT)
         p_rows[l] = p
-        wide_out[l] = wide_left(dot(p, inverses[l], precision=HIGHEST))
+        wide_out[l] = wide_left(dot(wide_left(p), tall_inverse))
         share = rows // (xs * ys)
         p_new[l] = p_rows[l, pl.ds(pl.multiple_of(col * share, 8), share), :]
-        q_new[l] = dot(inverses[l], opened(qg[1, l, row]), precision=HIGHEST)
+        q_new[l] = dot(wide_left(inverse), tall_right(opened(qg[1, row, l])))
     for copy in sent:
         copy.wait_send()
     sent.clear()
@@ -382,9 +402,8 @@
             pltpu.VMEM(q_prev.shape, F32),
             pltpu.VMEM(p_prev.shape, F32),
             pltpu.VMEM((layers, rows, cols), BF16),
-            pltpu.VMEM((layers, rows, cols), BF16),
-            pltpu.VMEM((layers, rows, cols), BF16),
-            pltpu.VMEM((2, layers, 2 * zs, wire, 128), F32),
+            pltpu.VMEM((layers, 2 * rows, cols), BF16),
+            pltpu.VMEM((2, 2 * zs, layers, wire, 128), F32),
             pltpu.VMEM((xs, ys, layers, 8, 128), F32),
             pltpu.VMEM((layers, rows, rank), F32),
             pltpu.VMEM((layers, rows, 6 * rank), BF16),

time: 51.7 us -> 49.2 us (0.952)
  Pallas kernels: 51 us -> 48.4 us
    pallas_call x1, Pallas kernels: 48.5 us -> 45.9 us  [shards(): pl.pallas_call(body, out_shape=(jax.ShapeDtypeStruct((layers, rows, cols)...]
where the time goes in v3:
time: 49.2 us; the launch traced here: 49.1 us
  Pallas kernels  48.4 us (98%)
  between operations  0.64 us (1%)
    pallas_call x1, Pallas kernels, shards(): pl.pallas_call(body, out_shape=(jax.ShapeDtypeStruct((layers, rows, cols)...  45.9 us
    pallas_call x1, Pallas kernels, shards(): pl.pallas_call(error_kernel, out_shape=(jax.ShapeDtypeStruct(p_prev.shape...  2.53 us

profile of v3, /device:TPU:1, one launch (start us, length us, event | category | flops | bytes accessed | tf_op | source)
XLA Modules:
  0.0 49.1 jit_solution(10051305651855452098)
XLA Ops:
  0.6 45.9 %factors.1 = (f32[2,384,1536]{2,1,0:T(8,128)S(1)}, bf16[2,384,192]{2,1,0:T(8,128)(2,1)S(1)}, f32[2,32,1536]{2,1,0:T(8,128)S(1)}, f32[2,24,32]{2,1,0:T(8,128)S(1)}, f32[2,32,96]{2,1,0:T(8,128)S(1)}) custom-call(bf16[2,384,1536]{2,1,0:T(8,128)(2,1)} %refs_0_.1, f32[2,384,1536]{2,1,0:T(8,128)} %refs_1_.1, f32[2,24,32]{2,1,0:T(8,128)} %refs_2_.1, ...), custom_call_target="tpu_custom_call" | custom-call | tf_op jit(solution)/shard_map/factors/pallas_call | solution.py:390
  46.5 2.5 %error.1 = (f32[2,24,32]{2,1,0:T(8,128)}, f32[2,32,96]{2,1,0:T(8,128)}, f32[2,384,1536]{2,1,0:T(8,128)}) custom-call(f32[2,384,1536]{2,1,0:T(8,128)S(1)} %get-tuple-element.11.merged, bf16[2,384,192]{2,1,0:T(8,128)(2,1)S(1)} %get-tuple-element.12.wide, f32[2,32,1536]{2,1,0:T(8,128)S(1)} %get-tuple-element.13.right, f32[2,24,32]{2,1,0:T(8,128)S(1)} %get-tuple-element.14.p_in, ...), custom_call_target="tpu_custom_call" | custom-call | tf_op jit(solution)/shard_map/error/pallas_call | solution.py:443

commit v4 on v3

--- a/solution.py
+++ b/solution.py
@@ -337,7 +337,8 @@
         tall_inverse = tall_right(inverse)
         p = dot(wide[l], wide_right(inverse), NT)
         p_rows[l] = p
-        wide_out[l] = wide_left(dot(wide_left(p), tall_inverse))
+        side = wide_out if l else wide.at[0]
+        side[...] = wide_left(dot(wide_left(p), tall_inverse))
         share = rows // (xs * ys)
         p_new[l] = p_rows[l, pl.ds(pl.multiple_of(col * share, 8), share), :]
         q_new[l] = dot(wide_left(inverse), tall_right(opened(qg[1, row, l])))
@@ -346,32 +347,35 @@
     sent.clear()
     for l in range(layers):
         pass_on(1, l)
-    for l in range(layers):
-        all_passed(1, l)
-        right_out[l] = q_columns(1, l)
+    all_passed(1, 0)
+    tall[0] = tall_right(q_columns(1, 0))
+    for j in range(cols // step):
+        at = pl.ds(j * step, step)
+        tile[0, :, at] = tile[0, :, at] - dot(wide[0], tall[0, :, at])
+    all_passed(1, 1)
+    right_out[...] = q_columns(1, 1)
     for copy in sent:
         copy.wait_send()
 
 
 def error_kernel(merged, wide, right, p_in, q_in, p_new, q_new, error, buf, tall, out_sem, small_sem):
-    layers, rows, cols = buf.shape
-    step = 128
-    small = [
+    rows, cols = buf.shape
+    step = rows // 3
+    copies = [pltpu.make_async_copy(merged.at[0], error.at[0], small_sem.at[2])]
+    copies += [
         pltpu.make_async_copy(p_in, p_new, small_sem.at[0]),
         pltpu.make_async_copy(q_in, q_new, small_sem.at[1]),
     ]
-    for c in small:
+    for c in copies:
         c.start()
-    outs = []
-    for l in range(layers):
-        tall[...] = tall_right(right[l])
-        for i in range(rows // step):
-            at = pl.ds(i * step, step)
-            buf[l, at, :] = merged[l, at, :] - dot(wide[l, at, :], tall[...])
-            copy = pltpu.make_async_copy(buf.at[l, at, :], error.at[l, at, :], out_sem.at[l, i])
-            copy.start()
-            outs.append(copy)
-    for c in outs + small:
+    tall[...] = tall_right(right[...])
+    for i in range(3):
+        at = pl.ds(i * step, step)
+        buf[at, :] = merged[1, at, :] - dot(wide[at, :], tall[...])
+        copy = pltpu.make_async_copy(buf.at[at, :], error.at[1, at, :], out_sem.at[i])
+        copy.start()
+        copies.append(copy)
+    for c in copies:
         c.wait()
 
 
@@ -391,8 +395,8 @@
         body,
         out_shape=(
             jax.ShapeDtypeStruct((layers, rows, cols), F32),
-            jax.ShapeDtypeStruct((layers, rows, 6 * rank), BF16),
-            jax.ShapeDtypeStruct((layers, rank, cols), F32),
+            jax.ShapeDtypeStruct((rows, 6 * rank), BF16),
+            jax.ShapeDtypeStruct((rank, cols), F32),
             jax.ShapeDtypeStruct(p_prev.shape, F32),
             jax.ShapeDtypeStruct(q_prev.shape, F32),
         ),
@@ -450,10 +454,10 @@
         in_specs=[vmem] * 5,
         out_specs=(hbm,) * 3,
         scratch_shapes=[
-            pltpu.VMEM((layers, rows, cols), F32),
+            pltpu.VMEM((rows, cols), F32),
             pltpu.VMEM((6 * rank, cols), BF16),
-            dma((layers, rows // 128)),
-            dma((2,)),
+            dma((3,)),
+            dma((3,)),
         ],
         compiler_params=pltpu.CompilerParams(vmem_limit_bytes=32 * 1024 * 1024),
         name="error",

time: 49.2 us -> 48.9 us (level)
  no operation moved by 1% of the time
where the time goes in v4:
time: 48.9 us; the launch traced here: 48.8 us
  Pallas kernels  48.1 us (98%)
  between operations  0.64 us (1%)
    pallas_call x1, Pallas kernels, shards(): pl.pallas_call(body, out_shape=(jax.ShapeDtypeStruct((layers, rows, cols)...  45.9 us
    pallas_call x1, Pallas kernels, shards(): pl.pallas_call(error_kernel, out_shape=(jax.ShapeDtypeStruct(p_prev.shape...  2.25 us

profile of v4, /device:TPU:1, one launch (start us, length us, event | category | flops | bytes accessed | tf_op | source)
XLA Modules:
  0.0 48.8 jit_solution(16688456307372214036)
XLA Ops:
  0.6 45.9 %factors.1 = (f32[2,384,1536]{2,1,0:T(8,128)S(1)}, bf16[384,192]{1,0:T(8,128)(2,1)S(1)}, f32[32,1536]{1,0:T(8,128)S(1)}, f32[2,24,32]{2,1,0:T(8,128)S(1)}, f32[2,32,96]{2,1,0:T(8,128)S(1)}) custom-call(bf16[2,384,1536]{2,1,0:T(8,128)(2,1)} %refs_0_.1, f32[2,384,1536]{2,1,0:T(8,128)} %refs_1_.1, f32[2,24,32]{2,1,0:T(8,128)} %refs_2_.1, f32[2,32,96]{2,1,0:T(8,128)} %bitcast.2), custom_call_target="tpu_custom_call" | custom-call | tf_op jit(solution)/shard_map/factors/pallas_call | solution.py:394
  46.5 2.2 %error.1 = (f32[2,24,32]{2,1,0:T(8,128)}, f32[2,32,96]{2,1,0:T(8,128)}, f32[2,384,1536]{2,1,0:T(8,128)}) custom-call(f32[2,384,1536]{2,1,0:T(8,128)S(1)} %get-tuple-element.11.merged, bf16[384,192]{1,0:T(8,128)(2,1)S(1)} %get-tuple-element.12.wide, f32[32,1536]{1,0:T(8,128)S(1)} %get-tuple-element.13.right, f32[2,24,32]{2,1,0:T(8,128)S(1)} %get-tuple-element.14.p_in, ...), custom_call_target="tpu_custom_call" | custom-call | tf_op jit(solution)/shard_map/error/pallas_call | solution.py:447

commit v5 on v4

--- a/solution.py
+++ b/solution.py
@@ -224,7 +224,7 @@
     def exchange(buf, stage, l, h, along_y):
         n, me, peer = (ys, y, y_peer) if along_y else (xs, x, x_peer)
         mine = buf.at[l, h, me]
-        for d in range(1, n):
+        for d in sorted(range(1, n), key=lambda d: -min(d, n - d)):
             start(remote(mine, mine, b_send.at[stage, l, h, d], b_recv.at[stage, l, h, d], peer(d)))
 
     def arrived(buf, stage, l, h, along_y):
@@ -274,11 +274,16 @@
                 left[l, h * half + b * block : h * half + (b + 1) * block, :] = total[:, 32 * b : 32 * b + 32]
         t1, t2, t3 = (t.astype(BF16) for t in pieces(left[l].T))
         lhs = jnp.concatenate([t1, t2, t3], axis=0)
-        g = folded(dot(lhs, lhs, NT))
+        grams = dot(lhs, lhs, NT)
+        g = folded(grams)
         gd[l, core] = jnp.concatenate([g[8 * i : 8 * i + 8] for i in range(4)], axis=1)
         mine = gd.at[l, core]
         start(remote(mine, mine, gd_send.at[l], gd_recv.at[l], partner))
-        full = dot(lhs, split[l, 0:rows, :]) + dot(lhs, split[l, rows : 2 * rows, :])
+        fulls = []
+        for h in range(2):
+            at = pl.ds(h * cols // 2, cols // 2)
+            fulls.append(dot(lhs, split[l, 0:rows, at]) + dot(lhs, split[l, rows : 2 * rows, at]))
+        full = jnp.concatenate(fulls, axis=1)
         r = full[0:32] + full[32:64] + full[64:96]
         for s in range(2 * zs):
             rb[l, s % 2, s // 2] = shut(r[:, 96 * s : 96 * s + 96])

time: 48.9 us -> 49.1 us (level)
  no operation moved by 1% of the time
where the time goes in v5:
time: 49.1 us; the launch traced here: 49 us
  Pallas kernels  48.4 us (99%)
  between operations  0.64 us (1%)
    pallas_call x1, Pallas kernels, shards(): pl.pallas_call(body, out_shape=(jax.ShapeDtypeStruct((layers, rows, cols)...  46.2 us
    pallas_call x1, Pallas kernels, shards(): pl.pallas_call(error_kernel, out_shape=(jax.ShapeDtypeStruct(p_prev.shape...  2.25 us

profile of v5, /device:TPU:1, one launch (start us, length us, event | category | flops | bytes accessed | tf_op | source)
XLA Modules:
  0.0 49.0 jit_solution(12880950571856518295)
XLA Ops:
  0.6 46.2 %factors.1 = (f32[2,384,1536]{2,1,0:T(8,128)S(1)}, bf16[384,192]{1,0:T(8,128)(2,1)S(1)}, f32[32,1536]{1,0:T(8,128)S(1)}, f32[2,24,32]{2,1,0:T(8,128)S(1)}, f32[2,32,96]{2,1,0:T(8,128)S(1)}) custom-call(bf16[2,384,1536]{2,1,0:T(8,128)(2,1)} %refs_0_.1, f32[2,384,1536]{2,1,0:T(8,128)} %refs_1_.1, f32[2,24,32]{2,1,0:T(8,128)} %refs_2_.1, f32[2,32,96]{2,1,0:T(8,128)} %bitcast.2), custom_call_target="tpu_custom_call" | custom-call | tf_op jit(solution)/shard_map/factors/pallas_call | solution.py:399
  46.8 2.2 %error.1 = (f32[2,24,32]{2,1,0:T(8,128)}, f32[2,32,96]{2,1,0:T(8,128)}, f32[2,384,1536]{2,1,0:T(8,128)}) custom-call(f32[2,384,1536]{2,1,0:T(8,128)S(1)} %get-tuple-element.11.merged, bf16[384,192]{1,0:T(8,128)(2,1)S(1)} %get-tuple-element.12.wide, f32[32,1536]{1,0:T(8,128)S(1)} %get-tuple-element.13.right, f32[2,24,32]{2,1,0:T(8,128)S(1)} %get-tuple-element.14.p_in, ...), custom_call_target="tpu_custom_call" | custom-call | tf_op jit(solution)/shard_map/error/pallas_call | solution.py:452
